TPU v7x, 32 devices: a whole 2x2x4 slice. The times are simulated.
32 devices in a mesh: gx: 4 (over z), gy: 4 (over x, core), gz: 2 (over y).
Axes of the slice: x: 2, y: 2, z: 4, core: 2. Of those that a mesh axis runs over, the one named last changes fastest.
Arguments:
- krylov_basis: float32 [60, 16, 32, 256], P(None, 'gx', 'gy', 'gz'), may hold values from -6 to 6
- schur_vectors: float32 [60, 20], replicated, may hold values from -1 to 1, as said below
- next_vector: float32 [16, 32, 256], P('gx', 'gy', 'gz'), may hold values from -10 to 10
- diag_shift: float32 [16, 32, 256], P('gx', 'gy', 'gz'), may hold values from 0.25 to 2
- velocity: float32 [3, 16, 32, 256], P(None, 'gx', 'gy', 'gz'), may hold values from -1 to 1
Outputs:
- new_basis: float32 [24, 16, 32, 256], P(None, 'gx', 'gy', 'gz')
- hessenberg: float32 [24, 3], replicated
Inputs may be any that keep to these rules, and one draw needn't show every extreme that they name: `schur_vectors`: the columns are orthonormal.
All inputs are finite; a program needn't handle non-finite values.
Results may differ from a plain program's by a relative error of at most 0.0003.
Values sent between devices are 32-bit elements; how exact they have to be, the bound alone decides.
A program may use at most 64 MiB of HBM per device.

v0:
```python
import jax
import jax.numpy as jnp
from jax import lax
from jax.sharding import PartitionSpec as P

KEEP = 20
EXPAND = 3
ROWS = 24


def with_halo(value, sides, width):
    for axis, dim in sides:
        count, length = (lax.axis_size(axis), value.shape[dim])
        up = [(i, (i + 1) % count) for i in range(count - 1)]
        down = [(j, i) for i, j in up]
        last = lax.slice_in_dim(value, length - width, length, axis=dim)
        initial = lax.slice_in_dim(value, 0, width, axis=dim)
        before = lax.ppermute(last, axis, up)
        after = lax.ppermute(initial, axis, down)
        value = jnp.concatenate([before, value, after], axis=dim)
    return value


def combine_terms(
    field, x_ahead, x_behind, y_ahead, y_behind, z_ahead, z_behind, diag_shift, velocity
):
    neighbours = x_ahead + x_behind + y_ahead + y_behind + z_ahead + z_behind
    flow = (
        velocity[0] * (x_ahead - x_behind)
        + velocity[1] * (y_ahead - y_behind)
        + velocity[2] * (z_ahead - z_behind)
    )
    return (6.0 + diag_shift) * field - neighbours + 0.5 * flow


def operate_field(field, diag_shift, velocity):
    padded = with_halo(field, (("gx", 0), ("gy", 1), ("gz", 2)), 1)
    return combine_terms(
        field,
        padded[2:, 1:-1, 1:-1],
        padded[:-2, 1:-1, 1:-1],
        padded[1:-1, 2:, 1:-1],
        padded[1:-1, :-2, 1:-1],
        padded[1:-1, 1:-1, 2:],
        padded[1:-1, 1:-1, :-2],
        diag_shift,
        velocity,
    )


def per_device(krylov_basis, schur_vectors, next_vector, diag_shift, velocity):
    highest = lax.Precision.HIGHEST
    shape_local = next_vector.shape
    cell_count = (
        shape_local[0]
        * shape_local[1]
        * shape_local[2]
        * lax.axis_size("gx")
        * lax.axis_size("gy")
        * lax.axis_size("gz")
    )
    rotated = jnp.einsum("ik,ixyz->kxyz", schur_vectors, krylov_basis, precision=highest)
    columns = []
    starting = jnp.concatenate([rotated, next_vector[None]], axis=0)
    flat_start = starting.reshape(KEEP + 1, -1)
    gram_matrix = (
        lax.psum(jnp.dot(flat_start, flat_start.T, precision=highest), ("gx", "gy", "gz"))
        / cell_count
    )
    divisor = jnp.maximum(jnp.sqrt(gram_matrix[KEEP, KEEP]), 0.5)
    factor = jnp.ones((KEEP + 1,), jnp.float32).at[KEEP].set(1.0 / divisor)
    gram_matrix = gram_matrix * factor[:, None] * factor[None, :]
    vectors = jnp.concatenate([rotated, (next_vector / divisor)[None]], axis=0)
    for expansion in range(EXPAND):
        count = vectors.shape[0]
        flat_basis = vectors.reshape(count, -1)
        applied = operate_field(vectors[-1], diag_shift, velocity).reshape(-1)
        dotted, self_sum = lax.psum(
            (jnp.dot(flat_basis, applied, precision=highest), jnp.sum(applied * applied)),
            ("gx", "gy", "gz"),
        )
        first_coeffs = dotted / cell_count
        self_norm = self_sum / cell_count
        second_coeffs = first_coeffs - jnp.dot(gram_matrix, first_coeffs, precision=highest)
        total_coeffs = first_coeffs + second_coeffs
        partly = applied - jnp.dot(first_coeffs, flat_basis, precision=highest)
        cleaned = partly - jnp.dot(second_coeffs, flat_basis, precision=highest)
        length_sq = (
            self_norm
            - 2.0 * jnp.dot(total_coeffs, first_coeffs, precision=highest)
            + jnp.dot(
                total_coeffs,
                jnp.dot(gram_matrix, total_coeffs, precision=highest),
                precision=highest,
            )
        )
        length = jnp.sqrt(jnp.maximum(length_sq, 0.0))
        divisor = jnp.maximum(length, 0.5)
        column = jnp.zeros((ROWS,), jnp.float32)
        column = column.at[:count].set(total_coeffs).at[count].set(length)
        columns.append(column)
        newest = (cleaned / divisor).reshape(shape_local)
        vectors = jnp.concatenate([vectors, newest[None]], axis=0)
        intersect = (
            second_coeffs - jnp.dot(gram_matrix, second_coeffs, precision=highest)
        ) / divisor
        corner = jnp.maximum(length_sq, 0.0) / (divisor * divisor)
        upper_rows = jnp.concatenate([gram_matrix, intersect[:, None]], axis=1)
        lower_row = jnp.concatenate([intersect, corner[None]], axis=0)
        gram_matrix = jnp.concatenate([upper_rows, lower_row[None]], axis=0)
    return (vectors, jnp.stack(columns, axis=1))


def solution(mesh):
    in_specs = (
        P(None, "gx", "gy", "gz"),
        P(),
        P("gx", "gy", "gz"),
        P("gx", "gy", "gz"),
        P(None, "gx", "gy", "gz"),
    )
    out_specs = (P(None, "gx", "gy", "gz"), P())
    return jax.shard_map(
        per_device, mesh=mesh, in_specs=in_specs, out_specs=out_specs, check_vma=False
    )
```

profile of v0, /device:TPU:0, one launch (start us, length us, event | category | flops | bytes accessed | tf_op | source)
XLA Modules:
  0.0 258.3 jit_solution(9260418553971904028)
XLA Ops:
  0.7 1.2 copy-done
  1.8 1.9 fusion.10
  3.7 0.5 convolution_bitcast_fusion
  4.2 42.1 %psum.49 = f32[21,21]{1,0:T(8,128)S(1)} all-reduce(f32[21,21]{1,0:T(8,128)S(1)} %convolution_bitcast_fusion), channel_id=1, replica_groups=mesh['gx'=4,'gy'=4,'gz'=2] {'gx','gy','gz'}, use_global_device_ids=true, to_apply=%region_0.0 | all-reduce | flops 441 | bytes 3528 | tf_op jit(solution)/shard_map/psum | solution.py:67
  46.3 0.6 slice.304
  47.6 1.3 collective-permute-start
  48.9 4.5 %collective-permute-start.1 = (f32[1,8,128]{2,1,0:T(8,128)S(1)}, f32[1,8,128]{2,1,0:T(8,128)S(1)}, u32[]{:S(2)}, u32[]{:S(2)}) collective-permute-start(f32[1,8,128]{2,1,0:T(8,128)S(1)} %get-tuple-element.124), channel_id=1, source_target_pairs={{0,8},{8,16},{16,24},{1,9},{9,17},{17,25},{2,10},{10,18},{18,26},{... | collective-permute-start | bytes 12296 | tf_op jit(solution)/shard_map/ppermute | solution.py:18
  53.7 1.1 collective-permute-done.1
  54.8 1.3 collective-permute-start.2
  56.1 3.0 %collective-permute-start.3 = (f32[6,1,128]{2,1,0:T(1,128)S(1)}, f32[6,1,128]{2,1,0:T(1,128)S(1)}, u32[]{:S(2)}, u32[]{:S(2)}) collective-permute-start(f32[6,1,128]{2,1,0:T(1,128)S(1)} %get-tuple-element.118), channel_id=1, source_target_pairs={{0,2},{2,4},{4,6},{1,3},{3,5},{5,7},{8,10},{10,12},{12,14},{9,11},... | collective-permute-start | bytes 9224 | tf_op jit(solution)/shard_map/ppermute | solution.py:18
  59.3 0.7 collective-permute-done.3
  60.0 4.2 %collective-permute-start.5 = (f32[6,10,1]{2,1,0:T(8,128)S(1)}, f32[6,10,1]{2,1,0:T(8,128)S(1)}, u32[]{:S(2)}, u32[]{:S(2)}) collective-permute-start(f32[6,10,1]{2,1,0:T(8,128)S(1)} %get-tuple-element.113), channel_id=1, source_target_pairs={{0,1},{2,3},{4,5},{6,7},{8,9},{10,11},{12,13},{14,15},{16,17},{18,... | collective-permute-start | bytes 728 | tf_op jit(solution)/shard_map/ppermute | solution.py:18
  64.2 1.3 collective-permute-start.4
  66.0 4.3 %collective-permute-done.4 = f32[6,10,1]{2,1,0:T(8,128)S(1)} collective-permute-done((f32[6,10,1]{2,1,0:T(8,128)S(1)}, f32[6,10,1]{2,1,0:T(8,128)S(1)}, u32[]{:S(2)}, u32[]{:S(2)}) %collective-permute-start.4) | collective-permute-done | bytes 272 | tf_op jit(solution)/shard_map/ppermute | solution.py:19
  70.2 0.7 multiply_reduce_fusion.2
  70.9 0.5 convolution_bitcast_fusion.11
  71.4 40.6 %all-reduce.6 = (f32[21]{0:T(128)S(1)}, f32[]{:T(128)}) all-reduce(f32[21]{0:T(128)S(1)} %convolution_bitcast_fusion.11, f32[]{:T(128)} %get-tuple-element.106), channel_id=1, replica_groups=mesh['gx'=4,'gy'=4,'gz'=2] {'gx','gy','gz'}, use_global_device_ids=true, to_apply=%region_1.0 | all-reduce | flops 22 | bytes 176 | tf_op jit(solution)/shard_map/psum | solution.py:78
  112.0 0.7 multiply_reduce_fusion.5
  114.1 0.7 fusion.12
  116.3 1.3 collective-permute-start.6
  117.6 4.5 %collective-permute-start.7 = (f32[1,8,128]{2,1,0:T(8,128)S(1)}, f32[1,8,128]{2,1,0:T(8,128)S(1)}, u32[]{:S(2)}, u32[]{:S(2)}) collective-permute-start(f32[1,8,128]{2,1,0:T(8,128)S(1)} %get-tuple-element.122), channel_id=1, source_target_pairs={{0,8},{8,16},{16,24},{1,9},{9,17},{17,25},{2,10},{10,18},{18,26},{... | collective-permute-start | bytes 12296 | tf_op jit(solution)/shard_map/ppermute | solution.py:18
  122.5 1.0 collective-permute-done.7
  123.5 1.3 collective-permute-start.8
  124.8 3.0 %collective-permute-start.9 = (f32[6,1,128]{2,1,0:T(1,128)S(1)}, f32[6,1,128]{2,1,0:T(1,128)S(1)}, u32[]{:S(2)}, u32[]{:S(2)}) collective-permute-start(f32[6,1,128]{2,1,0:T(1,128)S(1)} %get-tuple-element.116), channel_id=1, source_target_pairs={{0,2},{2,4},{4,6},{1,3},{3,5},{5,7},{8,10},{10,12},{12,14},{9,11},... | collective-permute-start | bytes 9224 | tf_op jit(solution)/shard_map/ppermute | solution.py:18
  127.8 0.8 collective-permute-done.9
  128.7 4.4 %collective-permute-start.11 = (f32[6,10,1]{2,1,0:T(8,128)S(1)}, f32[6,10,1]{2,1,0:T(8,128)S(1)}, u32[]{:S(2)}, u32[]{:S(2)}) collective-permute-start(f32[6,10,1]{2,1,0:T(8,128)S(1)} %get-tuple-element.111), channel_id=1, source_target_pairs={{0,1},{2,3},{4,5},{6,7},{8,9},{10,11},{12,13},{14,15},{16,17},{18,... | collective-permute-start | bytes 728 | tf_op jit(solution)/shard_map/ppermute | solution.py:18
  133.1 1.3 collective-permute-start.10
  134.8 4.5 %collective-permute-done.10 = f32[6,10,1]{2,1,0:T(8,128)S(1)} collective-permute-done((f32[6,10,1]{2,1,0:T(8,128)S(1)}, f32[6,10,1]{2,1,0:T(8,128)S(1)}, u32[]{:S(2)}, u32[]{:S(2)}) %collective-permute-start.10) | collective-permute-done | bytes 272 | tf_op jit(solution)/shard_map/ppermute | solution.py:19
  139.4 0.7 multiply_reduce_fusion.1
  140.5 41.6 %all-reduce.5 = (f32[22]{0:T(128)S(1)}, f32[]{:T(128)}) all-reduce(f32[22]{0:T(128)S(1)} %convolution_bitcast_fusion.10, f32[]{:T(128)} %get-tuple-element.102), channel_id=1, replica_groups=mesh['gx'=4,'gy'=4,'gz'=2] {'gx','gy','gz'}, use_global_device_ids=true, to_apply=%region_4.0 | all-reduce | flops 23 | bytes 184 | tf_op jit(solution)/shard_map/psum | solution.py:78
  182.1 0.7 multiply_reduce_fusion.4
  184.9 0.7 fusion.13
  186.5 1.3 collective-permute-start.12
  187.8 4.5 %collective-permute-start.13 = (f32[1,8,128]{2,1,0:T(8,128)S(1)}, f32[1,8,128]{2,1,0:T(8,128)S(1)}, u32[]{:S(2)}, u32[]{:S(2)}) collective-permute-start(f32[1,8,128]{2,1,0:T(8,128)S(1)} %get-tuple-element.120), channel_id=1, source_target_pairs={{0,8},{8,16},{16,24},{1,9},{9,17},{17,25},{2,10},{10,18},{18,26},{... | collective-permute-start | bytes 12296 | tf_op jit(solution)/shard_map/ppermute | solution.py:18
  192.6 1.0 collective-permute-done.13
  193.7 1.3 collective-permute-start.14
  195.0 3.0 %collective-permute-start.15 = (f32[6,1,128]{2,1,0:T(1,128)S(1)}, f32[6,1,128]{2,1,0:T(1,128)S(1)}, u32[]{:S(2)}, u32[]{:S(2)}) collective-permute-start(f32[6,1,128]{2,1,0:T(1,128)S(1)} %get-tuple-element.114), channel_id=1, source_target_pairs={{0,2},{2,4},{4,6},{1,3},{3,5},{5,7},{8,10},{10,12},{12,14},{9,11},... | collective-permute-start | bytes 9224 | tf_op jit(solution)/shard_map/ppermute | solution.py:18
  198.0 0.8 collective-permute-done.15
  198.9 4.4 %collective-permute-start.17 = (f32[6,10,1]{2,1,0:T(8,128)S(1)}, f32[6,10,1]{2,1,0:T(8,128)S(1)}, u32[]{:S(2)}, u32[]{:S(2)}) collective-permute-start(f32[6,10,1]{2,1,0:T(8,128)S(1)} %get-tuple-element.109), channel_id=1, source_target_pairs={{0,1},{2,3},{4,5},{6,7},{8,9},{10,11},{12,13},{14,15},{16,17},{18,... | collective-permute-start | bytes 728 | tf_op jit(solution)/shard_map/ppermute | solution.py:18
  203.3 1.3 collective-permute-start.16
  205.0 4.5 %collective-permute-done.16 = f32[6,10,1]{2,1,0:T(8,128)S(1)} collective-permute-done((f32[6,10,1]{2,1,0:T(8,128)S(1)}, f32[6,10,1]{2,1,0:T(8,128)S(1)}, u32[]{:S(2)}, u32[]{:S(2)}) %collective-permute-start.16) | collective-permute-done | bytes 272 | tf_op jit(solution)/shard_map/ppermute | solution.py:19
  209.5 0.7 multiply_reduce_fusion
  210.2 0.5 convolution_bitcast_fusion.9
  210.7 41.6 %all-reduce.4 = (f32[23]{0:T(128)S(1)}, f32[]{:T(128)}) all-reduce(f32[23]{0:T(128)S(1)} %convolution_bitcast_fusion.9, f32[]{:T(128)} %get-tuple-element.98), channel_id=1, replica_groups=mesh['gx'=4,'gy'=4,'gz'=2] {'gx','gy','gz'}, use_global_device_ids=true, to_apply=%region_7.0 | all-reduce | flops 24 | bytes 192 | tf_op jit(solution)/shard_map/psum | solution.py:78
  252.3 0.7 multiply_reduce_fusion.3
  253.0 0.8 fusion.14
  256.8 0.8 copy.15
  257.7 0.6 pad_maximum_fusion.77
  (60 shorter events, 5.6 us)
Async XLA Ops:
  0.6 1.2 copy-start
  0.6 3.1 %copy-start.3 = (f32[4,8,128]{2,1,0:T(8,128)S(1)}, f32[4,8,128]{2,1,0:T(8,128)}, u32[]{:S(2)}) copy-start(f32[4,8,128]{2,1,0:T(8,128)} %param.21) | copy-start | bytes 49156
  47.6 6.1 %collective-permute-start = (f32[1,8,128]{2,1,0:T(8,128)S(1)}, f32[1,8,128]{2,1,0:T(8,128)S(1)}, u32[]{:S(2)}, u32[]{:S(2)}) collective-permute-start(f32[1,8,128]{2,1,0:T(8,128)S(1)} %get-tuple-element.125), channel_id=1, source_target_pairs={{8,0},{16,8},{24,16},{9,1},{17,9},{25,17},{10,2},{18,10},{26,18},{... | collective-permute-start | bytes 12296 | tf_op jit(solution)/shard_map/ppermute | solution.py:19
  48.9 5.9 %collective-permute-start.1 = (f32[1,8,128]{2,1,0:T(8,128)S(1)}, f32[1,8,128]{2,1,0:T(8,128)S(1)}, u32[]{:S(2)}, u32[]{:S(2)}) collective-permute-start(f32[1,8,128]{2,1,0:T(8,128)S(1)} %get-tuple-element.124), channel_id=1, source_target_pairs={{0,8},{8,16},{16,24},{1,9},{9,17},{17,25},{2,10},{10,18},{18,26},{... | collective-permute-start | bytes 12296 | tf_op jit(solution)/shard_map/ppermute | solution.py:18
  54.8 4.5 %collective-permute-start.2 = (f32[6,1,128]{2,1,0:T(1,128)S(1)}, f32[6,1,128]{2,1,0:T(1,128)S(1)}, u32[]{:S(2)}, u32[]{:S(2)}) collective-permute-start(f32[6,1,128]{2,1,0:T(1,128)S(1)} %get-tuple-element.119), channel_id=1, source_target_pairs={{2,0},{4,2},{6,4},{3,1},{5,3},{7,5},{10,8},{12,10},{14,12},{11,9},... | collective-permute-start | bytes 9224 | tf_op jit(solution)/shard_map/ppermute | solution.py:19
  56.1 3.8 %collective-permute-start.3 = (f32[6,1,128]{2,1,0:T(1,128)S(1)}, f32[6,1,128]{2,1,0:T(1,128)S(1)}, u32[]{:S(2)}, u32[]{:S(2)}) collective-permute-start(f32[6,1,128]{2,1,0:T(1,128)S(1)} %get-tuple-element.118), channel_id=1, source_target_pairs={{0,2},{2,4},{4,6},{1,3},{3,5},{5,7},{8,10},{10,12},{12,14},{9,11},... | collective-permute-start | bytes 9224 | tf_op jit(solution)/shard_map/ppermute | solution.py:18
  60.0 5.9 %collective-permute-start.5 = (f32[6,10,1]{2,1,0:T(8,128)S(1)}, f32[6,10,1]{2,1,0:T(8,128)S(1)}, u32[]{:S(2)}, u32[]{:S(2)}) collective-permute-start(f32[6,10,1]{2,1,0:T(8,128)S(1)} %get-tuple-element.113), channel_id=1, source_target_pairs={{0,1},{2,3},{4,5},{6,7},{8,9},{10,11},{12,13},{14,15},{16,17},{18,... | collective-permute-start | bytes 728 | tf_op jit(solution)/shard_map/ppermute | solution.py:18
  64.2 6.0 %collective-permute-start.4 = (f32[6,10,1]{2,1,0:T(8,128)S(1)}, f32[6,10,1]{2,1,0:T(8,128)S(1)}, u32[]{:S(2)}, u32[]{:S(2)}) collective-permute-start(f32[6,10,1]{2,1,0:T(8,128)S(1)} %get-tuple-element.112), channel_id=1, source_target_pairs={{1,0},{3,2},{5,4},{7,6},{9,8},{11,10},{13,12},{15,14},{17,16},{19,... | collective-permute-start | bytes 728 | tf_op jit(solution)/shard_map/ppermute | solution.py:19
  65.6 4.6 %copy-start.1 = (f32[3,4,8,128]{3,2,1,0:T(8,128)S(1)}, f32[3,4,8,128]{3,2,1,0:T(8,128)}, u32[]{:S(2)}) copy-start(f32[3,4,8,128]{3,2,1,0:T(8,128)} %param.23) | copy-start | bytes 147460
  65.6 4.6 %copy-start.2 = (f32[4,8,128]{2,1,0:T(8,128)S(1)}, f32[4,8,128]{2,1,0:T(8,128)}, u32[]{:S(2)}) copy-start(f32[4,8,128]{2,1,0:T(8,128)} %param.22) | copy-start | bytes 49156
  116.3 6.2 %collective-permute-start.6 = (f32[1,8,128]{2,1,0:T(8,128)S(1)}, f32[1,8,128]{2,1,0:T(8,128)S(1)}, u32[]{:S(2)}, u32[]{:S(2)}) collective-permute-start(f32[1,8,128]{2,1,0:T(8,128)S(1)} %get-tuple-element.123), channel_id=1, source_target_pairs={{8,0},{16,8},{24,16},{9,1},{17,9},{25,17},{10,2},{18,10},{26,18},{... | collective-permute-start | bytes 12296 | tf_op jit(solution)/shard_map/ppermute | solution.py:19
  117.6 5.9 %collective-permute-start.7 = (f32[1,8,128]{2,1,0:T(8,128)S(1)}, f32[1,8,128]{2,1,0:T(8,128)S(1)}, u32[]{:S(2)}, u32[]{:S(2)}) collective-permute-start(f32[1,8,128]{2,1,0:T(8,128)S(1)} %get-tuple-element.122), channel_id=1, source_target_pairs={{0,8},{8,16},{16,24},{1,9},{9,17},{17,25},{2,10},{10,18},{18,26},{... | collective-permute-start | bytes 12296 | tf_op jit(solution)/shard_map/ppermute | solution.py:18
  123.5 4.3 %collective-permute-start.8 = (f32[6,1,128]{2,1,0:T(1,128)S(1)}, f32[6,1,128]{2,1,0:T(1,128)S(1)}, u32[]{:S(2)}, u32[]{:S(2)}) collective-permute-start(f32[6,1,128]{2,1,0:T(1,128)S(1)} %get-tuple-element.117), channel_id=1, source_target_pairs={{2,0},{4,2},{6,4},{3,1},{5,3},{7,5},{10,8},{12,10},{14,12},{11,9},... | collective-permute-start | bytes 9224 | tf_op jit(solution)/shard_map/ppermute | solution.py:19
  124.8 3.8 %collective-permute-start.9 = (f32[6,1,128]{2,1,0:T(1,128)S(1)}, f32[6,1,128]{2,1,0:T(1,128)S(1)}, u32[]{:S(2)}, u32[]{:S(2)}) collective-permute-start(f32[6,1,128]{2,1,0:T(1,128)S(1)} %get-tuple-element.116), channel_id=1, source_target_pairs={{0,2},{2,4},{4,6},{1,3},{3,5},{5,7},{8,10},{10,12},{12,14},{9,11},... | collective-permute-start | bytes 9224 | tf_op jit(solution)/shard_map/ppermute | solution.py:18
  128.7 6.1 %collective-permute-start.11 = (f32[6,10,1]{2,1,0:T(8,128)S(1)}, f32[6,10,1]{2,1,0:T(8,128)S(1)}, u32[]{:S(2)}, u32[]{:S(2)}) collective-permute-start(f32[6,10,1]{2,1,0:T(8,128)S(1)} %get-tuple-element.111), channel_id=1, source_target_pairs={{0,1},{2,3},{4,5},{6,7},{8,9},{10,11},{12,13},{14,15},{16,17},{18,... | collective-permute-start | bytes 728 | tf_op jit(solution)/shard_map/ppermute | solution.py:18
  133.1 6.3 %collective-permute-start.10 = (f32[6,10,1]{2,1,0:T(8,128)S(1)}, f32[6,10,1]{2,1,0:T(8,128)S(1)}, u32[]{:S(2)}, u32[]{:S(2)}) collective-permute-start(f32[6,10,1]{2,1,0:T(8,128)S(1)} %get-tuple-element.110), channel_id=1, source_target_pairs={{1,0},{3,2},{5,4},{7,6},{9,8},{11,10},{13,12},{15,14},{17,16},{19,... | collective-permute-start | bytes 728 | tf_op jit(solution)/shard_map/ppermute | solution.py:19
  186.5 6.2 %collective-permute-start.12 = (f32[1,8,128]{2,1,0:T(8,128)S(1)}, f32[1,8,128]{2,1,0:T(8,128)S(1)}, u32[]{:S(2)}, u32[]{:S(2)}) collective-permute-start(f32[1,8,128]{2,1,0:T(8,128)S(1)} %get-tuple-element.121), channel_id=1, source_target_pairs={{8,0},{16,8},{24,16},{9,1},{17,9},{25,17},{10,2},{18,10},{26,18},{... | collective-permute-start | bytes 12296 | tf_op jit(solution)/shard_map/ppermute | solution.py:19
  187.8 5.9 %collective-permute-start.13 = (f32[1,8,128]{2,1,0:T(8,128)S(1)}, f32[1,8,128]{2,1,0:T(8,128)S(1)}, u32[]{:S(2)}, u32[]{:S(2)}) collective-permute-start(f32[1,8,128]{2,1,0:T(8,128)S(1)} %get-tuple-element.120), channel_id=1, source_target_pairs={{0,8},{8,16},{16,24},{1,9},{9,17},{17,25},{2,10},{10,18},{18,26},{... | collective-permute-start | bytes 12296 | tf_op jit(solution)/shard_map/ppermute | solution.py:18
  193.7 4.3 %collective-permute-start.14 = (f32[6,1,128]{2,1,0:T(1,128)S(1)}, f32[6,1,128]{2,1,0:T(1,128)S(1)}, u32[]{:S(2)}, u32[]{:S(2)}) collective-permute-start(f32[6,1,128]{2,1,0:T(1,128)S(1)} %get-tuple-element.115), channel_id=1, source_target_pairs={{2,0},{4,2},{6,4},{3,1},{5,3},{7,5},{10,8},{12,10},{14,12},{11,9},... | collective-permute-start | bytes 9224 | tf_op jit(solution)/shard_map/ppermute | solution.py:19
  195.0 3.8 %collective-permute-start.15 = (f32[6,1,128]{2,1,0:T(1,128)S(1)}, f32[6,1,128]{2,1,0:T(1,128)S(1)}, u32[]{:S(2)}, u32[]{:S(2)}) collective-permute-start(f32[6,1,128]{2,1,0:T(1,128)S(1)} %get-tuple-element.114), channel_id=1, source_target_pairs={{0,2},{2,4},{4,6},{1,3},{3,5},{5,7},{8,10},{10,12},{12,14},{9,11},... | collective-permute-start | bytes 9224 | tf_op jit(solution)/shard_map/ppermute | solution.py:18
  198.9 6.1 %collective-permute-start.17 = (f32[6,10,1]{2,1,0:T(8,128)S(1)}, f32[6,10,1]{2,1,0:T(8,128)S(1)}, u32[]{:S(2)}, u32[]{:S(2)}) collective-permute-start(f32[6,10,1]{2,1,0:T(8,128)S(1)} %get-tuple-element.109), channel_id=1, source_target_pairs={{0,1},{2,3},{4,5},{6,7},{8,9},{10,11},{12,13},{14,15},{16,17},{18,... | collective-permute-start | bytes 728 | tf_op jit(solution)/shard_map/ppermute | solution.py:18
  203.3 6.3 %collective-permute-start.16 = (f32[6,10,1]{2,1,0:T(8,128)S(1)}, f32[6,10,1]{2,1,0:T(8,128)S(1)}, u32[]{:S(2)}, u32[]{:S(2)}) collective-permute-start(f32[6,10,1]{2,1,0:T(8,128)S(1)} %get-tuple-element.108), channel_id=1, source_target_pairs={{1,0},{3,2},{5,4},{7,6},{9,8},{11,10},{13,12},{15,14},{17,16},{19,... | collective-permute-start | bytes 728 | tf_op jit(solution)/shard_map/ppermute | solution.py:19
where the time goes:
time: 260 us; the launch traced here: 258 us
  blocking collectives  166 us (64%)
  starting transfers between devices  47.2 us (18%)
  waiting for transfers between devices  19.5 us (8%)
  matrix products  10.7 us (4%)
  between operations  7.79 us (3%)
  local copies, waits for them, and re-layouts  4 us (2%)
  other arithmetic  3.24 us (1%)
    psum x3, blocking collectives, per_device(): lax.psum((jnp.dot(flat_basis, applied, precision=highest), jnp.sum(applie...  124 us
    psum x1, blocking collectives, per_device(): lax.psum(jnp.dot(flat_start, flat_start.T, precision=highest), ('gx', 'gy...  42.1 us
    ppermute x9, starting transfers between devices, with_halo(): before = lax.ppermute(last, axis, up)  35.6 us
    ppermute x9, waiting for transfers between devices, with_halo(): after = lax.ppermute(initial, axis, down)  13.4 us
    ppermute x9, starting transfers between devices, with_halo(): after = lax.ppermute(initial, axis, down)  11.6 us
    ppermute x9, waiting for transfers between devices, with_halo(): before = lax.ppermute(last, axis, up)  6.12 us
  transfers between devices with their start and end apart: 18, of which 12 were waited for; matrix products, arithmetic and copies ran while one was open for 0% of the time, Pallas kernels for 0%

commit v1 on v0

--- a/solution.py
+++ b/solution.py
@@ -76,8 +76,11 @@
         flat_basis = vectors.reshape(count, -1)
         applied = operate_field(vectors[-1], diag_shift, velocity).reshape(-1)
         dotted, self_sum = lax.psum(
-            (jnp.dot(flat_basis, applied, precision=highest), jnp.sum(applied * applied)),
-            ("gx", "gy", "gz"),
+            lax.psum(
+                (jnp.dot(flat_basis, applied, precision=highest), jnp.sum(applied * applied)),
+                ("gy", "gz"),
+            ),
+            "gx",
         )
         first_coeffs = dotted / cell_count
         self_norm = self_sum / cell_count

time: 260 us -> 211 us (0.81)
  blocking collectives: 166 us -> 119 us
    psum x3, blocking collectives: 124 us -> 41 us  [per_device(): lax.psum((jnp.dot(flat_basis, applied, precision=highest), jnp.sum(applie...]
    psum x0 -> x3, blocking collectives: none -> 35.5 us  [per_device(): lax.psum(lax.psum((jnp.dot(flat_basis, applied, precision=highest), jnp.s...]
  transfers between devices with their start and end apart: 18 -> 18, of which waited for: 12 -> 12; matrix products, arithmetic and copies ran while one was open for 0% -> 1% of each run, Pallas kernels for 0% -> 0%
where the time goes in v1:
time: 211 us; the launch traced here: 210 us
  blocking collectives  119 us (56%)
  starting transfers between devices  46.8 us (22%)
  waiting for transfers between devices  19.1 us (9%)
  matrix products  10.7 us (5%)
  between operations  7.84 us (4%)
  local copies, waits for them, and re-layouts  4 us (2%)
  other arithmetic  3.24 us (2%)
    psum x1, blocking collectives, per_device(): lax.psum(jnp.dot(flat_start, flat_start.T, precision=highest), ('gx', 'gy...  42.1 us
    psum x3, blocking collectives, per_device(): lax.psum((jnp.dot(flat_basis, applied, precision=highest), jnp.sum(applie...  41 us
    psum x3, blocking collectives, per_device(): lax.psum(lax.psum((jnp.dot(flat_basis, applied, precision=highest), jnp.s...  35.5 us
    ppermute x9, starting transfers between devices, with_halo(): before = lax.ppermute(last, axis, up)  35.2 us
    ppermute x9, waiting for transfers between devices, with_halo(): after = lax.ppermute(initial, axis, down)  13 us
    ppermute x9, starting transfers between devices, with_halo(): after = lax.ppermute(initial, axis, down)  11.6 us
    ppermute x9, waiting for transfers between devices, with_halo(): before = lax.ppermute(last, axis, up)  6.12 us
  transfers between devices with their start and end apart: 18, of which 12 were waited for; matrix products, arithmetic and copies ran while one was open for 1% of the time, Pallas kernels for 0%

profile of v1, /device:TPU:0, one launch (start us, length us, event | category | flops | bytes accessed | tf_op | source)
XLA Modules:
  0.0 210.3 jit_solution(16777343644042464563)
XLA Ops:
  0.7 1.2 copy-done
  1.8 1.9 fusion.10
  4.2 42.1 %psum.91 = f32[21,21]{1,0:T(8,128)S(1)} all-reduce(f32[21,21]{1,0:T(8,128)S(1)} %convolution_bitcast_fusion), channel_id=1, replica_groups=mesh['gx'=4,'gy'=4,'gz'=2] {'gx','gy','gz'}, use_global_device_ids=true, to_apply=%region_0.0 | all-reduce | flops 441 | bytes 3528 | tf_op jit(solution)/shard_map/psum | solution.py:67
  46.3 0.6 slice.304
  47.6 1.3 collective-permute-start
  48.9 4.5 %collective-permute-start.1 = (f32[1,8,128]{2,1,0:T(8,128)S(1)}, f32[1,8,128]{2,1,0:T(8,128)S(1)}, u32[]{:S(2)}, u32[]{:S(2)}) collective-permute-start(f32[1,8,128]{2,1,0:T(8,128)S(1)} %get-tuple-element.130), channel_id=1, source_target_pairs={{0,8},{8,16},{16,24},{1,9},{9,17},{17,25},{2,10},{10,18},{18,26},{... | collective-permute-start | bytes 12296 | tf_op jit(solution)/shard_map/ppermute | solution.py:18
  53.7 1.1 collective-permute-done.1
  54.8 1.3 collective-permute-start.2
  56.1 3.0 %collective-permute-start.3 = (f32[6,1,128]{2,1,0:T(1,128)S(1)}, f32[6,1,128]{2,1,0:T(1,128)S(1)}, u32[]{:S(2)}, u32[]{:S(2)}) collective-permute-start(f32[6,1,128]{2,1,0:T(1,128)S(1)} %get-tuple-element.124), channel_id=1, source_target_pairs={{0,2},{2,4},{4,6},{1,3},{3,5},{5,7},{8,10},{10,12},{12,14},{9,11},... | collective-permute-start | bytes 9224 | tf_op jit(solution)/shard_map/ppermute | solution.py:18
  59.3 0.7 collective-permute-done.3
  60.0 4.2 %collective-permute-start.5 = (f32[6,10,1]{2,1,0:T(8,128)S(1)}, f32[6,10,1]{2,1,0:T(8,128)S(1)}, u32[]{:S(2)}, u32[]{:S(2)}) collective-permute-start(f32[6,10,1]{2,1,0:T(8,128)S(1)} %get-tuple-element.119), channel_id=1, source_target_pairs={{0,1},{2,3},{4,5},{6,7},{8,9},{10,11},{12,13},{14,15},{16,17},{18,... | collective-permute-start | bytes 728 | tf_op jit(solution)/shard_map/ppermute | solution.py:18
  64.2 1.3 collective-permute-start.4
  66.0 4.3 %collective-permute-done.4 = f32[6,10,1]{2,1,0:T(8,128)S(1)} collective-permute-done((f32[6,10,1]{2,1,0:T(8,128)S(1)}, f32[6,10,1]{2,1,0:T(8,128)S(1)}, u32[]{:S(2)}, u32[]{:S(2)}) %collective-permute-start.4) | collective-permute-done | bytes 272 | tf_op jit(solution)/shard_map/ppermute | solution.py:19
  70.2 0.7 multiply_reduce_fusion.2
  71.4 12.6 %all-reduce.6 = (f32[21]{0:T(128)S(1)}, f32[]{:T(128)}) all-reduce(f32[21]{0:T(128)S(1)} %convolution_bitcast_fusion.11, f32[]{:T(128)} %get-tuple-element.112), channel_id=1, replica_groups=mesh['gx'=4,'gy'=4,'gz'=2] {'gy','gz'}, use_global_device_ids=true, to_apply=%region_1.0 | all-reduce | flops 22 | bytes 176 | tf_op jit(solution)/shard_map/psum | solution.py:79
  84.0 13.0 %all-reduce.9 = (f32[21]{0:T(128)S(1)}, f32[]{:T(128)}) all-reduce(f32[21]{0:T(128)S(1)} %get-tuple-element.94, f32[]{:T(128)} %get-tuple-element.95), channel_id=1, replica_groups=mesh['gx'=4,'gy'=4,'gz'=2] {'gx'}, use_global_device_ids=true, to_apply=%region_2.0 | all-reduce | flops 22 | bytes 176 | tf_op jit(solution)/shard_map/psum | solution.py:78
  97.0 0.7 multiply_reduce_fusion.5
  99.1 0.7 fusion.12
  101.3 1.3 collective-permute-start.6
  102.6 4.5 %collective-permute-start.7 = (f32[1,8,128]{2,1,0:T(8,128)S(1)}, f32[1,8,128]{2,1,0:T(8,128)S(1)}, u32[]{:S(2)}, u32[]{:S(2)}) collective-permute-start(f32[1,8,128]{2,1,0:T(8,128)S(1)} %get-tuple-element.128), channel_id=1, source_target_pairs={{0,8},{8,16},{16,24},{1,9},{9,17},{17,25},{2,10},{10,18},{18,26},{... | collective-permute-start | bytes 12296 | tf_op jit(solution)/shard_map/ppermute | solution.py:18
  107.5 1.0 collective-permute-done.7
  108.5 1.3 collective-permute-start.8
  109.8 3.0 %collective-permute-start.9 = (f32[6,1,128]{2,1,0:T(1,128)S(1)}, f32[6,1,128]{2,1,0:T(1,128)S(1)}, u32[]{:S(2)}, u32[]{:S(2)}) collective-permute-start(f32[6,1,128]{2,1,0:T(1,128)S(1)} %get-tuple-element.122), channel_id=1, source_target_pairs={{0,2},{2,4},{4,6},{1,3},{3,5},{5,7},{8,10},{10,12},{12,14},{9,11},... | collective-permute-start | bytes 9224 | tf_op jit(solution)/shard_map/ppermute | solution.py:18
  112.9 0.8 collective-permute-done.9
  113.7 4.1 %collective-permute-start.11 = (f32[6,10,1]{2,1,0:T(8,128)S(1)}, f32[6,10,1]{2,1,0:T(8,128)S(1)}, u32[]{:S(2)}, u32[]{:S(2)}) collective-permute-start(f32[6,10,1]{2,1,0:T(8,128)S(1)} %get-tuple-element.117), channel_id=1, source_target_pairs={{0,1},{2,3},{4,5},{6,7},{8,9},{10,11},{12,13},{14,15},{16,17},{18,... | collective-permute-start | bytes 728 | tf_op jit(solution)/shard_map/ppermute | solution.py:18
  117.8 1.3 collective-permute-start.10
  119.6 4.3 %collective-permute-done.10 = f32[6,10,1]{2,1,0:T(8,128)S(1)} collective-permute-done((f32[6,10,1]{2,1,0:T(8,128)S(1)}, f32[6,10,1]{2,1,0:T(8,128)S(1)}, u32[]{:S(2)}, u32[]{:S(2)}) %collective-permute-start.10) | collective-permute-done | bytes 272 | tf_op jit(solution)/shard_map/ppermute | solution.py:19
  123.8 0.7 multiply_reduce_fusion.1
  125.0 14.4 %all-reduce.5 = (f32[22]{0:T(128)S(1)}, f32[]{:T(128)}) all-reduce(f32[22]{0:T(128)S(1)} %convolution_bitcast_fusion.10, f32[]{:T(128)} %get-tuple-element.108), channel_id=1, replica_groups=mesh['gx'=4,'gy'=4,'gz'=2] {'gy','gz'}, use_global_device_ids=true, to_apply=%region_6.0 | all-reduce | flops 23 | bytes 184 | tf_op jit(solution)/shard_map/psum | solution.py:79
  139.4 11.2 %all-reduce.8 = (f32[22]{0:T(128)S(1)}, f32[]{:T(128)}) all-reduce(f32[22]{0:T(128)S(1)} %get-tuple-element.92, f32[]{:T(128)} %get-tuple-element.93), channel_id=1, replica_groups=mesh['gx'=4,'gy'=4,'gz'=2] {'gx'}, use_global_device_ids=true, to_apply=%region_7.0 | all-reduce | flops 23 | bytes 184 | tf_op jit(solution)/shard_map/psum | solution.py:78
  150.7 0.7 multiply_reduce_fusion.4
  153.4 0.7 fusion.13
  155.0 1.3 collective-permute-start.12
  156.3 4.5 %collective-permute-start.13 = (f32[1,8,128]{2,1,0:T(8,128)S(1)}, f32[1,8,128]{2,1,0:T(8,128)S(1)}, u32[]{:S(2)}, u32[]{:S(2)}) collective-permute-start(f32[1,8,128]{2,1,0:T(8,128)S(1)} %get-tuple-element.126), channel_id=1, source_target_pairs={{0,8},{8,16},{16,24},{1,9},{9,17},{17,25},{2,10},{10,18},{18,26},{... | collective-permute-start | bytes 12296 | tf_op jit(solution)/shard_map/ppermute | solution.py:18
  161.2 1.0 collective-permute-done.13
  162.2 1.3 collective-permute-start.14
  163.5 3.0 %collective-permute-start.15 = (f32[6,1,128]{2,1,0:T(1,128)S(1)}, f32[6,1,128]{2,1,0:T(1,128)S(1)}, u32[]{:S(2)}, u32[]{:S(2)}) collective-permute-start(f32[6,1,128]{2,1,0:T(1,128)S(1)} %get-tuple-element.120), channel_id=1, source_target_pairs={{0,2},{2,4},{4,6},{1,3},{3,5},{5,7},{8,10},{10,12},{12,14},{9,11},... | collective-permute-start | bytes 9224 | tf_op jit(solution)/shard_map/ppermute | solution.py:18
  166.5 0.8 collective-permute-done.15
  167.4 4.2 %collective-permute-start.17 = (f32[6,10,1]{2,1,0:T(8,128)S(1)}, f32[6,10,1]{2,1,0:T(8,128)S(1)}, u32[]{:S(2)}, u32[]{:S(2)}) collective-permute-start(f32[6,10,1]{2,1,0:T(8,128)S(1)} %get-tuple-element.115), channel_id=1, source_target_pairs={{0,1},{2,3},{4,5},{6,7},{8,9},{10,11},{12,13},{14,15},{16,17},{18,... | collective-permute-start | bytes 728 | tf_op jit(solution)/shard_map/ppermute | solution.py:18
  171.6 1.3 collective-permute-start.16
  173.3 4.4 %collective-permute-done.16 = f32[6,10,1]{2,1,0:T(8,128)S(1)} collective-permute-done((f32[6,10,1]{2,1,0:T(8,128)S(1)}, f32[6,10,1]{2,1,0:T(8,128)S(1)}, u32[]{:S(2)}, u32[]{:S(2)}) %collective-permute-start.16) | collective-permute-done | bytes 272 | tf_op jit(solution)/shard_map/ppermute | solution.py:19
  177.8 0.7 multiply_reduce_fusion
  179.0 14.0 %all-reduce.4 = (f32[23]{0:T(128)S(1)}, f32[]{:T(128)}) all-reduce(f32[23]{0:T(128)S(1)} %convolution_bitcast_fusion.9, f32[]{:T(128)} %get-tuple-element.104), channel_id=1, replica_groups=mesh['gx'=4,'gy'=4,'gz'=2] {'gy','gz'}, use_global_device_ids=true, to_apply=%region_11.0 | all-reduce | flops 24 | bytes 192 | tf_op jit(solution)/shard_map/psum | solution.py:79
  193.0 11.2 %all-reduce.7 = (f32[23]{0:T(128)S(1)}, f32[]{:T(128)}) all-reduce(f32[23]{0:T(128)S(1)} %get-tuple-element.90, f32[]{:T(128)} %get-tuple-element.91), channel_id=1, replica_groups=mesh['gx'=4,'gy'=4,'gz'=2] {'gx'}, use_global_device_ids=true, to_apply=%region_12.0 | all-reduce | flops 24 | bytes 192 | tf_op jit(solution)/shard_map/psum | solution.py:78
  204.2 0.7 multiply_reduce_fusion.3
  205.0 0.8 fusion.14
  208.8 0.8 copy.15
  209.7 0.6 pad_maximum_fusion.77
  (63 shorter events, 7.1 us)
Async XLA Ops:
  0.6 1.2 copy-start
  0.6 3.1 %copy-start.3 = (f32[4,8,128]{2,1,0:T(8,128)S(1)}, f32[4,8,128]{2,1,0:T(8,128)}, u32[]{:S(2)}) copy-start(f32[4,8,128]{2,1,0:T(8,128)} %param.21) | copy-start | bytes 49156
  47.6 6.1 %collective-permute-start = (f32[1,8,128]{2,1,0:T(8,128)S(1)}, f32[1,8,128]{2,1,0:T(8,128)S(1)}, u32[]{:S(2)}, u32[]{:S(2)}) collective-permute-start(f32[1,8,128]{2,1,0:T(8,128)S(1)} %get-tuple-element.131), channel_id=1, source_target_pairs={{8,0},{16,8},{24,16},{9,1},{17,9},{25,17},{10,2},{18,10},{26,18},{... | collective-permute-start | bytes 12296 | tf_op jit(solution)/shard_map/ppermute | solution.py:19
  48.9 5.9 %collective-permute-start.1 = (f32[1,8,128]{2,1,0:T(8,128)S(1)}, f32[1,8,128]{2,1,0:T(8,128)S(1)}, u32[]{:S(2)}, u32[]{:S(2)}) collective-permute-start(f32[1,8,128]{2,1,0:T(8,128)S(1)} %get-tuple-element.130), channel_id=1, source_target_pairs={{0,8},{8,16},{16,24},{1,9},{9,17},{17,25},{2,10},{10,18},{18,26},{... | collective-permute-start | bytes 12296 | tf_op jit(solution)/shard_map/ppermute | solution.py:18
  54.8 4.5 %collective-permute-start.2 = (f32[6,1,128]{2,1,0:T(1,128)S(1)}, f32[6,1,128]{2,1,0:T(1,128)S(1)}, u32[]{:S(2)}, u32[]{:S(2)}) collective-permute-start(f32[6,1,128]{2,1,0:T(1,128)S(1)} %get-tuple-element.125), channel_id=1, source_target_pairs={{2,0},{4,2},{6,4},{3,1},{5,3},{7,5},{10,8},{12,10},{14,12},{11,9},... | collective-permute-start | bytes 9224 | tf_op jit(solution)/shard_map/ppermute | solution.py:19
  56.1 3.8 %collective-permute-start.3 = (f32[6,1,128]{2,1,0:T(1,128)S(1)}, f32[6,1,128]{2,1,0:T(1,128)S(1)}, u32[]{:S(2)}, u32[]{:S(2)}) collective-permute-start(f32[6,1,128]{2,1,0:T(1,128)S(1)} %get-tuple-element.124), channel_id=1, source_target_pairs={{0,2},{2,4},{4,6},{1,3},{3,5},{5,7},{8,10},{10,12},{12,14},{9,11},... | collective-permute-start | bytes 9224 | tf_op jit(solution)/shard_map/ppermute | solution.py:18
  60.0 5.9 %collective-permute-start.5 = (f32[6,10,1]{2,1,0:T(8,128)S(1)}, f32[6,10,1]{2,1,0:T(8,128)S(1)}, u32[]{:S(2)}, u32[]{:S(2)}) collective-permute-start(f32[6,10,1]{2,1,0:T(8,128)S(1)} %get-tuple-element.119), channel_id=1, source_target_pairs={{0,1},{2,3},{4,5},{6,7},{8,9},{10,11},{12,13},{14,15},{16,17},{18,... | collective-permute-start | bytes 728 | tf_op jit(solution)/shard_map/ppermute | solution.py:18
  64.2 6.0 %collective-permute-start.4 = (f32[6,10,1]{2,1,0:T(8,128)S(1)}, f32[6,10,1]{2,1,0:T(8,128)S(1)}, u32[]{:S(2)}, u32[]{:S(2)}) collective-permute-start(f32[6,10,1]{2,1,0:T(8,128)S(1)} %get-tuple-element.118), channel_id=1, source_target_pairs={{1,0},{3,2},{5,4},{7,6},{9,8},{11,10},{13,12},{15,14},{17,16},{19,... | collective-permute-start | bytes 728 | tf_op jit(solution)/shard_map/ppermute | solution.py:19
  65.6 4.6 %copy-start.1 = (f32[3,4,8,128]{3,2,1,0:T(8,128)S(1)}, f32[3,4,8,128]{3,2,1,0:T(8,128)}, u32[]{:S(2)}) copy-start(f32[3,4,8,128]{3,2,1,0:T(8,128)} %param.23) | copy-start | bytes 147460
  65.6 4.6 %copy-start.2 = (f32[4,8,128]{2,1,0:T(8,128)S(1)}, f32[4,8,128]{2,1,0:T(8,128)}, u32[]{:S(2)}) copy-start(f32[4,8,128]{2,1,0:T(8,128)} %param.22) | copy-start | bytes 49156
  101.3 6.2 %collective-permute-start.6 = (f32[1,8,128]{2,1,0:T(8,128)S(1)}, f32[1,8,128]{2,1,0:T(8,128)S(1)}, u32[]{:S(2)}, u32[]{:S(2)}) collective-permute-start(f32[1,8,128]{2,1,0:T(8,128)S(1)} %get-tuple-element.129), channel_id=1, source_target_pairs={{8,0},{16,8},{24,16},{9,1},{17,9},{25,17},{10,2},{18,10},{26,18},{... | collective-permute-start | bytes 12296 | tf_op jit(solution)/shard_map/ppermute | solution.py:19
  102.6 5.9 %collective-permute-start.7 = (f32[1,8,128]{2,1,0:T(8,128)S(1)}, f32[1,8,128]{2,1,0:T(8,128)S(1)}, u32[]{:S(2)}, u32[]{:S(2)}) collective-permute-start(f32[1,8,128]{2,1,0:T(8,128)S(1)} %get-tuple-element.128), channel_id=1, source_target_pairs={{0,8},{8,16},{16,24},{1,9},{9,17},{17,25},{2,10},{10,18},{18,26},{... | collective-permute-start | bytes 12296 | tf_op jit(solution)/shard_map/ppermute | solution.py:18
  108.5 4.3 %collective-permute-start.8 = (f32[6,1,128]{2,1,0:T(1,128)S(1)}, f32[6,1,128]{2,1,0:T(1,128)S(1)}, u32[]{:S(2)}, u32[]{:S(2)}) collective-permute-start(f32[6,1,128]{2,1,0:T(1,128)S(1)} %get-tuple-element.123), channel_id=1, source_target_pairs={{2,0},{4,2},{6,4},{3,1},{5,3},{7,5},{10,8},{12,10},{14,12},{11,9},... | collective-permute-start | bytes 9224 | tf_op jit(solution)/shard_map/ppermute | solution.py:19
  109.8 3.8 %collective-permute-start.9 = (f32[6,1,128]{2,1,0:T(1,128)S(1)}, f32[6,1,128]{2,1,0:T(1,128)S(1)}, u32[]{:S(2)}, u32[]{:S(2)}) collective-permute-start(f32[6,1,128]{2,1,0:T(1,128)S(1)} %get-tuple-element.122), channel_id=1, source_target_pairs={{0,2},{2,4},{4,6},{1,3},{3,5},{5,7},{8,10},{10,12},{12,14},{9,11},... | collective-permute-start | bytes 9224 | tf_op jit(solution)/shard_map/ppermute | solution.py:18
  113.7 5.8 %collective-permute-start.11 = (f32[6,10,1]{2,1,0:T(8,128)S(1)}, f32[6,10,1]{2,1,0:T(8,128)S(1)}, u32[]{:S(2)}, u32[]{:S(2)}) collective-permute-start(f32[6,10,1]{2,1,0:T(8,128)S(1)} %get-tuple-element.117), channel_id=1, source_target_pairs={{0,1},{2,3},{4,5},{6,7},{8,9},{10,11},{12,13},{14,15},{16,17},{18,... | collective-permute-start | bytes 728 | tf_op jit(solution)/shard_map/ppermute | solution.py:18
  117.8 6.0 %collective-permute-start.10 = (f32[6,10,1]{2,1,0:T(8,128)S(1)}, f32[6,10,1]{2,1,0:T(8,128)S(1)}, u32[]{:S(2)}, u32[]{:S(2)}) collective-permute-start(f32[6,10,1]{2,1,0:T(8,128)S(1)} %get-tuple-element.116), channel_id=1, source_target_pairs={{1,0},{3,2},{5,4},{7,6},{9,8},{11,10},{13,12},{15,14},{17,16},{19,... | collective-permute-start | bytes 728 | tf_op jit(solution)/shard_map/ppermute | solution.py:19
  155.0 6.2 %collective-permute-start.12 = (f32[1,8,128]{2,1,0:T(8,128)S(1)}, f32[1,8,128]{2,1,0:T(8,128)S(1)}, u32[]{:S(2)}, u32[]{:S(2)}) collective-permute-start(f32[1,8,128]{2,1,0:T(8,128)S(1)} %get-tuple-element.127), channel_id=1, source_target_pairs={{8,0},{16,8},{24,16},{9,1},{17,9},{25,17},{10,2},{18,10},{26,18},{... | collective-permute-start | bytes 12296 | tf_op jit(solution)/shard_map/ppermute | solution.py:19
  156.3 5.9 %collective-permute-start.13 = (f32[1,8,128]{2,1,0:T(8,128)S(1)}, f32[1,8,128]{2,1,0:T(8,128)S(1)}, u32[]{:S(2)}, u32[]{:S(2)}) collective-permute-start(f32[1,8,128]{2,1,0:T(8,128)S(1)} %get-tuple-element.126), channel_id=1, source_target_pairs={{0,8},{8,16},{16,24},{1,9},{9,17},{17,25},{2,10},{10,18},{18,26},{... | collective-permute-start | bytes 12296 | tf_op jit(solution)/shard_map/ppermute | solution.py:18
  162.2 4.3 %collective-permute-start.14 = (f32[6,1,128]{2,1,0:T(1,128)S(1)}, f32[6,1,128]{2,1,0:T(1,128)S(1)}, u32[]{:S(2)}, u32[]{:S(2)}) collective-permute-start(f32[6,1,128]{2,1,0:T(1,128)S(1)} %get-tuple-element.121), channel_id=1, source_target_pairs={{2,0},{4,2},{6,4},{3,1},{5,3},{7,5},{10,8},{12,10},{14,12},{11,9},... | collective-permute-start | bytes 9224 | tf_op jit(solution)/shard_map/ppermute | solution.py:19
  163.5 3.8 %collective-permute-start.15 = (f32[6,1,128]{2,1,0:T(1,128)S(1)}, f32[6,1,128]{2,1,0:T(1,128)S(1)}, u32[]{:S(2)}, u32[]{:S(2)}) collective-permute-start(f32[6,1,128]{2,1,0:T(1,128)S(1)} %get-tuple-element.120), channel_id=1, source_target_pairs={{0,2},{2,4},{4,6},{1,3},{3,5},{5,7},{8,10},{10,12},{12,14},{9,11},... | collective-permute-start | bytes 9224 | tf_op jit(solution)/shard_map/ppermute | solution.py:18
  167.4 5.9 %collective-permute-start.17 = (f32[6,10,1]{2,1,0:T(8,128)S(1)}, f32[6,10,1]{2,1,0:T(8,128)S(1)}, u32[]{:S(2)}, u32[]{:S(2)}) collective-permute-start(f32[6,10,1]{2,1,0:T(8,128)S(1)} %get-tuple-element.115), channel_id=1, source_target_pairs={{0,1},{2,3},{4,5},{6,7},{8,9},{10,11},{12,13},{14,15},{16,17},{18,... | collective-permute-start | bytes 728 | tf_op jit(solution)/shard_map/ppermute | solution.py:18
  171.6 6.2 %collective-permute-start.16 = (f32[6,10,1]{2,1,0:T(8,128)S(1)}, f32[6,10,1]{2,1,0:T(8,128)S(1)}, u32[]{:S(2)}, u32[]{:S(2)}) collective-permute-start(f32[6,10,1]{2,1,0:T(8,128)S(1)} %get-tuple-element.114), channel_id=1, source_target_pairs={{1,0},{3,2},{5,4},{7,6},{9,8},{11,10},{13,12},{15,14},{17,16},{19,... | collective-permute-start | bytes 728 | tf_op jit(solution)/shard_map/ppermute | solution.py:19
